TPU v7x, 64 devices: a 2x2x8 block of a 4x4x8 slice. The times are simulated.
64 devices in a mesh: dp: 4 (over x, y), ep: 16 (over z, core).
Axes of the slice: x: 2, y: 2, z: 8, core: 2. Of those that a mesh axis runs over, the one named last changes fastest.
The devices are a block of a 4x4x8 slice.
Arguments:
- x_in: bfloat16 [65536, 1024], P(('dp', 'ep')), parts along dimension 0
- norm_gain: bfloat16 [1024], replicated
- w_router: bfloat16 [1024, 32], replicated
- expert_ids: int32 [65536, 8], P(('dp', 'ep')), parts along dimension 0
- w_gate: bfloat16 [32, 1024, 512], P('ep')
- w_up: bfloat16 [32, 1024, 512], P('ep')
- w_down: bfloat16 [32, 512, 1024], P('ep')
Outputs:
- output: bfloat16 [65536, 1024], P(('dp', 'ep')), parts along dimension 0
There are 4 independent parts. A program takes and returns all parts, laid end to end along the dimension named above; an argument that names none is the same for every part.
All inputs are finite; a program needn't handle non-finite values.
Results may differ from a plain program's by a relative error of at most 0.001.
Values are sent between devices in bfloat16 or wider.
A program may use at most 768 MiB of HBM per device.

v0:
```python
import jax
import jax.numpy as jnp
from jax import lax
from jax.sharding import PartitionSpec as P

EPS = 1e-6


def norm_and_gates(x_in, norm_gain, w_router, expert_ids):
    resid = x_in.astype(jnp.float32)
    mean_sq = jnp.mean(resid * resid, axis=-1, keepdims=True)
    normed = (resid * lax.rsqrt(mean_sq + EPS) * norm_gain.astype(jnp.float32)).astype(jnp.bfloat16)
    logits = jnp.dot(normed, w_router, preferred_element_type=jnp.float32)
    router_p = jax.nn.softmax(logits, axis=-1)
    picked = jnp.take_along_axis(router_p, expert_ids, axis=1)
    gates = picked / jnp.sum(picked, axis=1, keepdims=True)
    return resid, normed, gates


def route_slots(expert_ids, experts, capacity):
    flat_ids = expert_ids.reshape(-1)
    onehot = (flat_ids[:, None] == jnp.arange(experts, dtype=jnp.int32)[None, :]).astype(jnp.int32)
    before = jnp.cumsum(onehot, axis=0) - onehot
    position = jnp.sum(before * onehot, axis=1)
    return flat_ids * capacity + position


def expert_mlp(rows, w_gate, w_up, w_down):
    gate_val = jnp.einsum("erd,edf->erf", rows, w_gate, preferred_element_type=jnp.float32)
    up_val = jnp.einsum("erd,edf->erf", rows, w_up, preferred_element_type=jnp.float32)
    hidden_act = (jax.nn.silu(gate_val) * up_val).astype(jnp.bfloat16)
    return jnp.einsum("erf,efd->erd", hidden_act, w_down, preferred_element_type=jnp.float32).astype(jnp.bfloat16)


def solution(mesh):
    def local_block(x_in, norm_gain, w_router, expert_ids, w_gate, w_up, w_down):
        tokens, hidden = x_in.shape
        experts = w_router.shape[1]
        top_k = expert_ids.shape[1]
        capacity = 2 * tokens * top_k // experts
        resid, normed, gates = norm_and_gates(x_in, norm_gain, w_router, expert_ids)
        slots = route_slots(expert_ids, experts, capacity)
        choice_tok = jnp.arange(tokens * top_k, dtype=jnp.int32) // top_k
        slot_tok = jnp.full((experts * capacity,), tokens, jnp.int32).at[slots].set(choice_tok)
        outgoing = jnp.take(normed, slot_tok, axis=0, mode="fill", fill_value=0).reshape(experts, capacity, hidden)
        received = lax.all_to_all(outgoing, "ep", 0, 1, tiled=True)
        outputs = expert_mlp(received, w_gate, w_up, w_down)
        returned = lax.all_to_all(outputs, "ep", 1, 0, tiled=True).reshape(experts * capacity, hidden)
        y_sel = jnp.take(returned, slots, axis=0).reshape(tokens, top_k, hidden)
        mixed = jnp.sum(y_sel.astype(jnp.float32) * gates[:, :, None], axis=1)
        return (resid + mixed).astype(jnp.bfloat16)

    tok_spec = P(("dp", "ep"), None)
    expert_spec = P("ep", None, None)
    return jax.shard_map(local_block, mesh=mesh, in_specs=(tok_spec, P(None), P(None, None), tok_spec, expert_spec, expert_spec, expert_spec), out_specs=tok_spec, check_vma=False)
```

profile of v0, /device:TPU:21, one launch (start us, length us, event | category | flops | bytes accessed | tf_op | source)
XLA Modules:
  0.0 2023.8 jit_solution(3806325185138271158)
XLA Ops:
  0.0 0.0 copy-start
  0.0 0.0 copy-start.12
  0.0 0.9 broadcast_multiply_fusion
  0.9 0.9 copy.32
  1.9 0.3 eq.26
  2.1 0.3 reshape.109
  2.4 0.2 copy.36
  2.6 0.3 mul.59
  2.9 1.1 fusion.10
  4.0 17.1 reduce-window.6
  21.1 0.9 slice_reduce_fusion
  22.0 0.2 reduce-window.9
  22.3 0.3 broadcast_add_fusion
  22.6 0.8 fusion.9
  23.4 0.0 copy-start.7
  23.4 0.1 compare_select_fusion
  23.5 0.6 copy-done.7
  24.0 0.0 copy-start.9
  24.0 30.5 %scatter_custom_fusion = s32[16384]{0:T(1024)S(1)} fusion(s32[8192]{0:T(1024)S(1)} %bitcast.57, s32[8192]{0:T(1024)S(1)} %add_select_fusion, s32[]{:T(128)} %constant.70.clone.1), kind=kCustom, calls=%fused_computation.43 | custom fusion | bytes 65540 | tf_op jit(solution)/shard_map/scatter | solution.py:44
  54.5 0.0 copy-done.9
  54.6 0.0 copy-done.12
  54.6 2.1 fusion.3
  56.7 3.5 fusion.5
  60.2 81.9 %gather_fusion = bf16[16384,1024]{1,0:T(8,128)(2,1)} fusion(bf16[1024,1024]{1,0:T(8,128)(2,1)} %fusion.5, s32[16384]{0:T(1024)S(1)} %fusion.13), kind=kCustom, calls=%fused_computation | custom fusion | bytes 67174400 | tf_op jit(solution)/shard_map/jit(_take)/gather | solution.py:45
  142.1 22.8 %broadcast_select_fusion = bf16[32,512,1024]{2,1,0:T(8,128)(2,1)} fusion(bf16[32,512,1024]{2,1,0:T(8,128)(2,1)} %bitcast.51, pred[32,512]{1,0:T(8,128)(4,1)S(1)} %broadcast_in_dim.41), kind=kLoop, calls=%fused_computation.6 | loop fusion | flops 16777216 | bytes 67125248 | tf_op jit(solution)/shard_map/jit(_take)/select_n | solution.py:45
  164.9 737.6 %all_to_all.33 = bf16[32,512,1024]{2,1,0:T(8,128)(2,1)} all-to-all(bf16[32,512,1024]{2,1,0:T(8,128)(2,1)} %broadcast_select_fusion), channel_id=1, replica_groups=mesh['dp'=4,'ep'=16] {'ep'}, dimensions={0} | all-to-all | bytes 67108864 | tf_op jit(solution)/shard_map/all_to_all | solution.py:46
  902.5 22.6 %copy.37 = bf16[2,16,512,1024]{3,2,1,0:T(8,128)(2,1)} copy(bf16[2,16,512,1024]{3,2,0,1:T(8,128)(2,1)} %bitcast.52) | data formatting | bytes 67108864 | tf_op jit(solution)/shard_map/all_to_all | solution.py:46
  925.2 32.2 %fusion.22 = f32[2,8192,512]{2,1,0:T(8,128)} fusion(bf16[2,8192,1024]{2,1,0:T(8,128)(2,1)} %bitcast.53, bf16[2,1024,512]{2,1,0:T(8,128)(2,1)} %param.11), kind=kOutput, calls=%fused_computation.55 | convolution fusion | flops 17179869184 | bytes 69206016 | tf_op jit(solution)/shard_map/erd,edf->erf/dot_general | solution.py:29
  957.4 0.0 copy-done
  957.4 47.4 %convolution_convert_fusion = bf16[2,8192,1024]{2,1,0:T(8,128)(2,1)} fusion(bf16[2,512,1024]{2,1,0:T(8,128)(2,1)S(1)} %copy-done, f32[2,8192,512]{2,1,0:T(8,128)} %fusion.22, bf16[2,8192,1024]{2,1,0:T(8,128)(2,1)} %bitcast.54, bf16[2,1024,512]{2,1,0:T(8,128)(2,1)} %param.12), kind=kOutput, calls=%fused_computation.7 | convolution fusion | flops 34426847232 | bytes 104857600 | tf_op jit(solution)/shard_map/erf,efd->erd/dot_general | solution.py:32
  1004.8 60.3 %copy.38 = bf16[2,8192,1024]{2,0,1:T(2,128)(2,1)} copy(bf16[2,8192,1024]{2,1,0:T(8,128)(2,1)} %convolution_convert_fusion) | data formatting | bytes 67108864 | tf_op jit(solution)/shard_map/convert_element_type | solution.py:32
  1065.1 0.0 copy-start.8
  1065.1 0.0 copy-start.4
  1065.1 0.0 copy-start.2
  1065.1 0.0 copy-start.11
  1065.2 7.7 all-to-all-start.1
  1072.8 0.0 copy-done.8
  1072.8 0.3 reduce_sum.50
  1073.1 0.0 copy-done.4
  1073.2 0.2 copy.40
  1073.4 0.3 reshape.129
  1073.6 0.2 copy.34
  1073.8 0.9 copy.35
  1074.7 0.0 copy-done.2
  1074.7 0.0 copy-done.11
  1074.7 0.7 fusion.21
  1075.5 0.0 copy-start.5
  1075.5 0.0 copy-start.10
  1075.5 65.5 %gather_fusion.2 = f32[8192]{0:T(1024)S(1)} fusion(f32[1024,32]{0,1:T(8,128)S(1)} %fusion.11, s32[8192]{0:T(1024)S(1)} %reshape.129), kind=kCustom, calls=%fused_computation.2 | custom fusion | bytes 131072 | tf_op jit(solution)/shard_map/jit(take_along_axis)/gather | solution.py:15
  1141.1 0.3 reshape.132
  1141.4 0.2 copy.41
  1141.5 0.0 copy-done.5
  1141.6 0.2 copy.42
  1141.8 0.0 copy-done.10
  1141.8 689.1 %all-to-all-done.1 = bf16[2,8192,1024]{2,0,1:T(2,128)(2,1)} async-done(((bf16[2,8192,1024]{2,0,1:T(2,128)(2,1)}), bf16[2,8192,1024]{2,0,1:T(2,128)(2,1)}, u32[]{:S(2)}, u32[]{:S(2)}) %all-to-all-start.1) | async-done | bytes 33554464 | tf_op jit(solution)/shard_map/all_to_all | solution.py:48
  1831.0 23.1 %copy.39 = bf16[2,16,512,1024]{3,2,0,1:T(8,128)(2,1)} copy(bf16[2,16,512,1024]{3,0,2,1:T(2,128)(2,1)} %bitcast.7) | data formatting | bytes 67108864 | tf_op jit(solution)/shard_map/all_to_all | solution.py:48
  1854.1 0.0 copy-start.6
  1854.1 150.4 %gather_fusion.1 = bf16[8192,1024]{1,0:T(8,128)(2,1)} fusion(bf16[16384,1024]{1,0:T(8,128)(2,1)} %bitcast.50, s32[8192]{0:T(1024)S(1)} %broadcast_clamp_fusion), kind=kCustom, calls=%fused_computation.1 | custom fusion | bytes 33587200 | tf_op jit(solution)/shard_map/jit(_take)/gather | solution.py:49
  2004.5 0.0 copy-done.6
  2004.5 0.0 copy-start.3
  2004.5 17.1 multiply_reduce_fusion
  2021.6 0.0 copy-done.3
  2021.6 2.1 fusion.6
  2023.8 0.0 copy-done.1
  (14 shorter events, 0.3 us)
Async XLA Ops:
  0.0 957.4 %copy-start = (bf16[2,512,1024]{2,1,0:T(8,128)(2,1)S(1)}, bf16[2,512,1024]{2,1,0:T(8,128)(2,1)}, u32[]{:S(2)}) copy-start(bf16[2,512,1024]{2,1,0:T(8,128)(2,1)} %param.13) | copy-start | bytes 6291460
  0.0 54.6 %copy-start.12 = (bf16[1024]{0:T(1024)(128)(2,1)S(1)}, bf16[1024]{0:T(1024)(128)(2,1)}, u32[]{:S(2)}) copy-start(bf16[1024]{0:T(1024)(128)(2,1)} %param.8) | copy-start | bytes 6148
  23.4 0.6 copy-start.7
  24.0 30.5 %copy-start.9 = (s32[8192,1]{0,1:T(1,128)}, s32[8192,1]{0,1:T(1,128)S(1)}, u32[]{:S(2)}) copy-start(s32[8192,1]{0,1:T(1,128)S(1)} %compare_select_fusion) | copy-start | bytes 98308
  1065.1 7.7 copy-start.8
  1065.1 8.0 copy-start.4
  1065.1 9.5 copy-start.2
  1065.1 9.5 copy-start.11
  1065.2 765.8 %all-to-all-start.1 = ((bf16[2,8192,1024]{2,0,1:T(2,128)(2,1)}), bf16[2,8192,1024]{2,0,1:T(2,128)(2,1)}, u32[]{:S(2)}, u32[]{:S(2)}) async-start(bf16[2,8192,1024]{2,0,1:T(2,128)(2,1)} %copy.38), calls=%async_computation.1 | async-start | bytes 67108864 | tf_op jit(solution)/shard_map/all_to_all | solution.py:48
  1075.5 66.0 %copy-start.5 = (s32[1024,8]{0,1:T(8,128)S(1)}, s32[1024,8]{0,1:T(8,128)}, u32[]{:S(2)}) copy-start(s32[1024,8]{0,1:T(8,128)} %param.10) | copy-start | bytes 98308
  1075.5 66.3 %copy-start.10 = (s32[8192,1]{0,1:T(1,128)S(1)}, s32[8192,1]{0,1:T(1,128)}, u32[]{:S(2)}) copy-start(s32[8192,1]{0,1:T(1,128)} %copy-done.9) | copy-start | bytes 98308
  1854.1 150.4 %copy-start.6 = (pred[1024,8]{1,0:T(8,128)(4,1)S(1)}, pred[1024,8]{1,0:T(8,128)(4,1)}, u32[]{:S(2)}) copy-start(pred[1024,8]{1,0:T(8,128)(4,1)} %copy.35) | copy-start | bytes 24580
  2004.5 17.1 copy-start.3
  2004.5 19.2 copy-start.1
where the time goes:
time: 2030 us; the launch traced here: 2020 us
  blocking collectives  738 us (36%)
  waiting for transfers between devices  689 us (34%)
  local copies, waits for them, and re-layouts  440 us (22%)
  matrix products  80.4 us (4%)
  other arithmetic  68.3 us (3%)
    all_to_all x1, blocking collectives, local_block(): received = lax.all_to_all(outgoing, 'ep', 0, 1, tiled=True)  738 us
    all_to_all x1, waiting for transfers between devices, local_block(): lax.all_to_all(outputs, 'ep', 1, 0, tiled=True)  689 us
    gather x1, local copies, waits for them, and re-layouts, local_block(): y_sel = jnp.take(returned, slots, axis=0).reshape(tokens, top_k, hidden)  150 us
    gather x1, local copies, waits for them, and re-layouts, local_block(): jnp.take(normed, slot_tok, axis=0, mode='fill', fill_value=0)  81.9 us
    gather x5, local copies, waits for them, and re-layouts, norm_and_gates(): picked = jnp.take_along_axis(router_p, expert_ids, axis=1)  66.4 us
    convert_element_type x1, local copies, waits for them, and re-layouts, expert_mlp(): jnp.einsum('erf,efd->erd', hidden_act, w_down, preferred_element_type=jnp...  60.3 us
    dot_general x1, matrix products, expert_mlp(): jnp.einsum('erf,efd->erd', hidden_act, w_down, preferred_element_type=jnp...  47.4 us
  transfers between devices with their start and end apart: 1, of which 1 were waited for; matrix products, arithmetic and copies ran while one was open for 3% of the time, Pallas kernels for 0%

commit v1 on v0

v1 whole, which is shorter than its diff:
```python
import functools
import math

import jax
import jax.numpy as jnp
from jax import lax
from jax.experimental import pallas as pl
from jax.experimental.pallas import tpu as pltpu
from jax.sharding import PartitionSpec as P

EPS = 1e-6
MESH = pl.DeviceIdType.MESH
LANES = 128
CORES = 2
LAG = 3


def kernel(nz, yspan, x_ref, gain_ref, router_ref, ids_ref, gate_in, up_in, down_in, out_ref, gate_land, up_land, down_land,
           normed, total, weight, hidden, gate_buf, up_buf, down_buf, send_z, send_xy, send_sib, recv, load_sem):
    dp, ep = lax.axis_index("dp"), lax.axis_index("ep")
    z, c = ep // CORES, ep % CORES
    a, b = (dp // yspan) % 2, dp % 2
    relay = (a + b + c) % 2
    right = (dp, ((z + 1) % nz) * CORES + c)
    left = (dp, ((z + nz - 1) % nz) * CORES + c)
    x_peer = (dp + yspan * (1 - 2 * a), ep)
    y_peer = (dp + 1 - 2 * b, ep)
    sibling = (dp, z * CORES + 1 - c)
    tokens, width = x_ref.shape
    experts = router_ref.shape[1]
    batches = nz - 1
    items = 4 * nz
    arrays = ((gate_in, gate_land, gate_buf), (up_in, up_land, up_buf), (down_in, down_land, down_buf))

    def send(src, dst, send_sem, recv_sem, device):
        return pltpu.make_async_remote_copy(src_ref=src, dst_ref=dst, send_sem=send_sem, recv_sem=recv_sem, device_id=device, device_id_type=MESH)

    barrier = pltpu.get_barrier_semaphore()
    for peer in (right, left, x_peer, y_peer, sibling):
        pl.semaphore_signal(barrier, inc=1, device_id=peer, device_id_type=MESH)
    pl.semaphore_wait(barrier, 5)

    for j in range(2):
        for k, (own, land, _) in enumerate(arrays):
            @pl.when(relay == 0)
            def _():
                send(own.at[j], land.at[c, z, j], send_z.at[0, k, j], recv.at[k, c, z, j], right).start()
                send(own.at[1 - j], land.at[c, z, 1 - j], send_z.at[1, k, j], recv.at[k, c, z, 1 - j], left).start()
            send(own.at[j], land.at[c, z, j], send_sib.at[k, 0, j], recv.at[k, c, z, j], sibling).start()

    tile = min(128, tokens)

    @pl.loop(0, tokens // tile)
    def _(step):
        rows = pl.ds(pl.multiple_of(step * tile, tile), tile)
        resid = x_ref[rows, :].astype(jnp.float32)
        mean_sq = jnp.mean(resid * resid, axis=-1, keepdims=True)
        row = (resid * lax.rsqrt(mean_sq + EPS) * gain_ref[...].astype(jnp.float32)).astype(jnp.bfloat16)
        normed[rows, :] = row
        total[rows, :] = resid
        logits = jnp.dot(row, router_ref[...], preferred_element_type=jnp.float32)
        ids = ids_ref[rows, :]
        lane = lax.broadcasted_iota(jnp.int32, (tile, experts), 1)
        chosen = lane == ids[:, 0:1]
        for j in range(1, ids.shape[1]):
            chosen = chosen | (lane == ids[:, j:j + 1])
        shifted = jnp.exp(logits - jnp.max(logits, axis=-1, keepdims=True))
        prob = shifted / jnp.sum(shifted, axis=-1, keepdims=True)
        picked = jnp.where(chosen, prob, 0.0)
        gates = picked / jnp.sum(picked, axis=-1, keepdims=True)
        for e in range(experts):
            weight[e, rows, :] = jnp.broadcast_to(gates[:, e:e + 1], (tile, LANES))

    def place(n, side):
        dist, first = 1 + n // 2, n % 2
        return (z + nz + (2 * side - 1) * dist) % nz, first + side - 2 * first * side

    def exchange(n, k):
        _, land, _ = arrays[k]
        first = n % 2
        for side in range(2):
            zs, j = place(n, side)
            chunk, sem = land.at[c, zs, j], recv.at[k, c, zs, j]
            send(chunk, chunk, send_sib.at[k, n + 1, side], sem, sibling).wait_recv()

            @pl.when((relay == 0) & (n < batches - 2))
            def _():
                send(chunk, chunk, send_z.at[side, k, n + 2], sem, (right, left)[side]).start()

            @pl.when((relay == 0) & (first == side))
            def _():
                send(chunk, chunk, send_xy.at[0, k, n], sem, x_peer).start()

            @pl.when((relay == 0) & (first != side))
            def _():
                send(chunk, chunk, send_xy.at[1, k, n], sem, y_peer).start()
            send(chunk, chunk, send_sib.at[k, n + 1, side], sem, sibling).start()

    @pl.loop(0, items)
    def _(i):
        at = i - LAG * relay
        live = (at >= 0) & (at < 4 * batches)
        for k, phase in enumerate((0, 2, 3)):
            @pl.when(live & ((at + 4) % 4 == phase))
            def _():
                exchange((at + 4) // 4 - 1, k)

        m, q = i // 4, i % 4
        side, other = q % 2, (q // 2 + relay) % 2
        cls = (c + other) % 2
        dist, first = (m + 1) // 2, (m + 1) % 2
        zs = (z + nz + (2 * side - 1) * dist) % nz
        j = first + side - 2 * first * side
        slot = i % 2

        @pl.when(other == 1)
        def _():
            for k, (_, land, _) in enumerate(arrays):
                chunk = land.at[cls, zs, j]
                send(chunk, chunk, send_sib.at[k, 0, 0], recv.at[k, cls, zs, j], sibling).wait_recv()

        native = (m == 0) & (other == 0)

        @pl.when(native)
        def _():
            for k, (own, _, buf) in enumerate(arrays):
                pltpu.make_async_copy(own.at[j], buf.at[slot], load_sem.at[k]).start()

        @pl.when(jnp.logical_not(native))
        def _():
            for k, (_, land, buf) in enumerate(arrays):
                pltpu.make_async_copy(land.at[cls, zs, j], buf.at[slot], load_sem.at[k]).start()

        for k in range(2):
            own, _, buf = arrays[k]
            pltpu.make_async_copy(own.at[0], buf.at[slot], load_sem.at[k]).wait()

        span = min(512, tokens)

        @pl.loop(0, tokens // span)
        def _(step):
            rows = pl.ds(pl.multiple_of(step * span, span), span)
            row = normed[rows, :]
            gate_val = jnp.dot(row, gate_buf[slot], preferred_element_type=jnp.float32)
            up_val = jnp.dot(row, up_buf[slot], preferred_element_type=jnp.float32)
            hidden[rows, :] = (jax.nn.silu(gate_val) * up_val).astype(jnp.bfloat16)

        pltpu.make_async_copy(down_in.at[0], down_buf.at[slot], load_sem.at[2]).wait()
        expert = (zs * CORES + cls) * 2 + j

        @pl.loop(0, tokens // span)
        def _(step):
            rows = pl.ds(pl.multiple_of(step * span, span), span)
            y = jnp.dot(hidden[rows, :], down_buf[slot], preferred_element_type=jnp.float32).astype(jnp.bfloat16).astype(jnp.float32)
            scale = jnp.concatenate([weight[expert, rows, :]] * (width // LANES), axis=1)
            total[rows, :] += jnp.where(scale != 0.0, scale * y, 0.0)

    @pl.loop(0, tokens // tile)
    def _(step):
        rows = pl.ds(pl.multiple_of(step * tile, tile), tile)
        out_ref[rows, :] = total[rows, :].astype(jnp.bfloat16)

    for k, (own, land, _) in enumerate(arrays):
        @pl.when(relay == 0)
        def _():
            @pl.loop(0, batches)
            def _(n):
                for side in range(2):
                    send(own.at[0], land.at[0, 0, 0], send_z.at[side, k, n], recv.at[k, 0, 0, 0], right).wait_send()
                    send(own.at[0], land.at[0, 0, 0], send_xy.at[side, k, n], recv.at[k, 0, 0, 0], right).wait_send()

        @pl.loop(0, batches + 1)
        def _(n):
            for side in range(2):
                send(own.at[0], land.at[0, 0, 0], send_sib.at[k, n, side], recv.at[k, 0, 0, 0], sibling).wait_send()


def solution(mesh):
    yspan = math.isqrt(mesh.shape["dp"])
    nz = mesh.shape["ep"] // CORES

    def local_block(x_in, norm_gain, w_router, expert_ids, w_gate, w_up, w_down):
        tokens, width = x_in.shape
        experts = w_router.shape[1]
        ff = w_gate.shape[2]
        batches = nz - 1
        vmem, anywhere = pl.BlockSpec(memory_space=pltpu.VMEM), pl.BlockSpec(memory_space=pl.ANY)
        land_in = jax.ShapeDtypeStruct((CORES, nz, 2, width, ff), jnp.bfloat16)
        land_out = jax.ShapeDtypeStruct((CORES, nz, 2, ff, width), jnp.bfloat16)
        dma = pltpu.SemaphoreType.DMA
        return pl.pallas_call(
            functools.partial(kernel, nz, yspan),
            out_shape=(jax.ShapeDtypeStruct(x_in.shape, x_in.dtype), land_in, land_in, land_out),
            in_specs=[vmem, vmem, vmem, vmem, anywhere, anywhere, anywhere],
            out_specs=(vmem, anywhere, anywhere, anywhere),
            scratch_shapes=[
                pltpu.VMEM((tokens, width), jnp.bfloat16),
                pltpu.VMEM((tokens, width), jnp.float32),
                pltpu.VMEM((experts, tokens, LANES), jnp.float32),
                pltpu.VMEM((tokens, ff), jnp.bfloat16),
                pltpu.VMEM((2, width, ff), jnp.bfloat16),
                pltpu.VMEM((2, width, ff), jnp.bfloat16),
                pltpu.VMEM((2, ff, width), jnp.bfloat16),
                dma((2, 3, batches)),
                dma((2, 3, batches)),
                dma((3, nz, 2)),
                dma((3, CORES, nz, 2)),
                dma((3,)),
            ],
            compiler_params=pltpu.CompilerParams(collective_id=0, has_side_effects=True, vmem_limit_bytes=60 * 1024 * 1024),
            name="moe",
        )(x_in, norm_gain.reshape(1, width), w_router, expert_ids, w_gate, w_up, w_down)[0]

    tok_spec = P(("dp", "ep"), None)
    expert_spec = P("ep", None, None)
    return jax.shard_map(local_block, mesh=mesh, in_specs=(tok_spec, P(None), P(None, None), tok_spec, expert_spec, expert_spec, expert_spec), out_specs=tok_spec, check_vma=False)
```

time: 2030 us -> 288 us (0.14)
  blocking collectives: 738 us -> 0 us
  waiting for transfers between devices: 689 us -> 0 us
  local copies, waits for them, and re-layouts: 440 us -> 7.79 us
  Pallas kernels: 0 us -> 278 us
  matrix products: 80.4 us -> 0 us
  other arithmetic: 68.3 us -> 0 us
    all_to_all x1 -> x0, blocking collectives: 738 us -> none  [local_block(): received = lax.all_to_all(outgoing, 'ep', 0, 1, tiled=True)]
    all_to_all x1 -> x0, waiting for transfers between devices: 689 us -> none  [local_block(): lax.all_to_all(outputs, 'ep', 1, 0, tiled=True)]
    gather x7 -> x0, local copies, waits for them, and re-layouts: 299 us -> none  [the longest x1 150 us: local_block(): y_sel = jnp.take(returned, slots, axis=0).reshape(tokens, top_k, hidden)]
    pallas_call x0 -> x1, Pallas kernels: none -> 278 us  [local_block(): pl.pallas_call(functools.partial(kernel, nz, yspan), out_shape=(jax.Shape...]
    dot_general x3 -> x0, matrix products: 80.4 us -> none  [the longest x1 47.4 us: expert_mlp(): jnp.einsum('erf,efd->erd', hidden_act, w_down, preferred_element_type=jnp...]
    convert_element_type x1 -> x0, local copies, waits for them, and re-layouts: 60.3 us -> none  [expert_mlp(): jnp.einsum('erf,efd->erd', hidden_act, w_down, preferred_element_type=jnp...]
    all_to_all x2 -> x0, local copies, waits for them, and re-layouts: 45.8 us -> none  [the longest x1 23.1 us: local_block(): lax.all_to_all(outputs, 'ep', 1, 0, tiled=True)]
    scatter x1 -> x0, local copies, waits for them, and re-layouts: 30.5 us -> none  [local_block(): jnp.full((experts * capacity,), tokens, jnp.int32).at[slots].set(choice_tok)]
  transfers between devices with their start and end apart: 1 -> 0, of which waited for: 1 -> 0; matrix products, arithmetic and copies ran while one was open for 3% -> 0% of each run, Pallas kernels for 0% -> 0%
where the time goes in v1:
time: 288 us; the launch traced here: 286 us
  Pallas kernels  278 us (97%)
  local copies, waits for them, and re-layouts  7.79 us (3%)
    pallas_call x1, Pallas kernels, local_block(): pl.pallas_call(functools.partial(kernel, nz, yspan), out_shape=(jax.Shape...  278 us
    unnamed x3, local copies, waits for them, and re-layouts  6.52 us

profile of v1, /device:TPU:21, one launch (start us, length us, event | category | flops | bytes accessed | tf_op | source)
XLA Modules:
  0.0 286.2 jit_solution(16039266395234349477)
XLA Ops:
  0.0 1.3 reshape.3.gain_ref
  1.3 1.7 copy.8.router_ref
  3.0 1.8 copy.9.ids_ref
  4.7 278.4 %moe.1 = (bf16[1024,1024]{1,0:T(8,128)(2,1)}, bf16[2,8,2,1024,512]{4,3,2,1,0:T(8,128)(2,1)}, bf16[2,8,2,1024,512]{4,3,2,1,0:T(8,128)(2,1)}, bf16[2,8,2,512,1024]{4,3,2,1,0:T(8,128)(2,1)}) custom-call(bf16[1024,1024]{1,0:T(8,128)(2,1)} %x_ref.1, bf16[1,1024]{1,0:T(2,128)(2,1)} %reshape.3.gain_ref, bf16[1024,32]{1,0:T(8,128)(2,1)} %copy.8.router_ref, ...), custom_call_target="tpu_custom_call" | custom-call | tf_op jit(solution)/shard_map/moe/pallas_call | solution.py:191
  283.1 3.1 %copy.11 = bf16[1024,1024]{1,0:T(8,128)(2,1)} copy(bf16[1024,1024]{1,0:T(8,128)(2,1)} %get-tuple-element.6) | data formatting | bytes 4194304

commit v2 on v1

--- a/solution.py
+++ b/solution.py
@@ -10,9 +10,9 @@
 
 EPS = 1e-6
 MESH = pl.DeviceIdType.MESH
-LANES = 128
 CORES = 2
-LAG = 3
+LAG_FROM_Z, LAG_FROM_XY = 2, 4
+DEFER = 2
 
 
 def kernel(nz, yspan, x_ref, gain_ref, router_ref, ids_ref, gate_in, up_in, down_in, out_ref, gate_land, up_land, down_land,
@@ -27,7 +27,7 @@
     y_peer = (dp + 1 - 2 * b, ep)
     sibling = (dp, z * CORES + 1 - c)
     tokens, width = x_ref.shape
-    experts = router_ref.shape[1]
+    experts = router_ref.shape[0]
     batches = nz - 1
     items = 4 * nz
     arrays = ((gate_in, gate_land, gate_buf), (up_in, up_land, up_buf), (down_in, down_land, down_buf))
@@ -55,21 +55,20 @@
         rows = pl.ds(pl.multiple_of(step * tile, tile), tile)
         resid = x_ref[rows, :].astype(jnp.float32)
         mean_sq = jnp.mean(resid * resid, axis=-1, keepdims=True)
-        row = (resid * lax.rsqrt(mean_sq + EPS) * gain_ref[...].astype(jnp.float32)).astype(jnp.bfloat16)
+        row = (resid * lax.rsqrt(mean_sq + EPS) * gain_ref[...].astype(jnp.float32).reshape(1, width)).astype(jnp.bfloat16)
         normed[rows, :] = row
         total[rows, :] = resid
-        logits = jnp.dot(row, router_ref[...], preferred_element_type=jnp.float32)
-        ids = ids_ref[rows, :]
-        lane = lax.broadcasted_iota(jnp.int32, (tile, experts), 1)
-        chosen = lane == ids[:, 0:1]
-        for j in range(1, ids.shape[1]):
-            chosen = chosen | (lane == ids[:, j:j + 1])
-        shifted = jnp.exp(logits - jnp.max(logits, axis=-1, keepdims=True))
-        prob = shifted / jnp.sum(shifted, axis=-1, keepdims=True)
+        logits = lax.dot_general(router_ref[...], row, (((1,), (1,)), ((), ())), preferred_element_type=jnp.float32)
+        ids = ids_ref[:, rows]
+        index = lax.broadcasted_iota(jnp.int32, (experts, tile), 0)
+        chosen = index == ids[0:1, :]
+        for j in range(1, ids.shape[0]):
+            chosen = chosen | (index == ids[j:j + 1, :])
+        shifted = jnp.exp(logits - jnp.max(logits, axis=0, keepdims=True))
+        prob = shifted / jnp.sum(shifted, axis=0, keepdims=True)
         picked = jnp.where(chosen, prob, 0.0)
-        gates = picked / jnp.sum(picked, axis=-1, keepdims=True)
-        for e in range(experts):
-            weight[e, rows, :] = jnp.broadcast_to(gates[:, e:e + 1], (tile, LANES))
+        gates = picked / jnp.sum(picked, axis=0, keepdims=True)
+        weight[rows, :] = gates.T
 
     def place(n, side):
         dist, first = 1 + n // 2, n % 2
@@ -96,64 +95,85 @@
                 send(chunk, chunk, send_xy.at[1, k, n], sem, y_peer).start()
             send(chunk, chunk, send_sib.at[k, n + 1, side], sem, sibling).start()
 
-    @pl.loop(0, items)
-    def _(i):
-        at = i - LAG * relay
-        live = (at >= 0) & (at < 4 * batches)
-        for k, phase in enumerate((0, 2, 3)):
-            @pl.when(live & ((at + 4) % 4 == phase))
-            def _():
-                exchange((at + 4) // 4 - 1, k)
-
+    @pl.when(relay == 0)
+    def _():
+        exchange(0, 0)
+
+    def locate(i):
         m, q = i // 4, i % 4
         side, other = q % 2, (q // 2 + relay) % 2
-        cls = (c + other) % 2
         dist, first = (m + 1) // 2, (m + 1) % 2
-        zs = (z + nz + (2 * side - 1) * dist) % nz
-        j = first + side - 2 * first * side
-        slot = i % 2
+        return other, (m == 0) & (other == 0), (c + other) % 2, (z + nz + (2 * side - 1) * dist) % nz, first + side - 2 * first * side
+
+    def fetch(i, which):
+        other, native, cls, zs, j = locate(i)
 
         @pl.when(other == 1)
         def _():
-            for k, (_, land, _) in enumerate(arrays):
-                chunk = land.at[cls, zs, j]
+            for k in which:
+                chunk = arrays[k][1].at[cls, zs, j]
                 send(chunk, chunk, send_sib.at[k, 0, 0], recv.at[k, cls, zs, j], sibling).wait_recv()
 
-        native = (m == 0) & (other == 0)
-
         @pl.when(native)
         def _():
-            for k, (own, _, buf) in enumerate(arrays):
-                pltpu.make_async_copy(own.at[j], buf.at[slot], load_sem.at[k]).start()
+            for k in which:
+                own, _, buf = arrays[k]
+                pltpu.make_async_copy(own.at[j], buf.at[i % 2], load_sem.at[k]).start()
 
         @pl.when(jnp.logical_not(native))
         def _():
-            for k, (_, land, buf) in enumerate(arrays):
-                pltpu.make_async_copy(land.at[cls, zs, j], buf.at[slot], load_sem.at[k]).start()
-
-        for k in range(2):
+            for k in which:
+                _, land, buf = arrays[k]
+                pltpu.make_async_copy(land.at[cls, zs, j], buf.at[i % 2], load_sem.at[k]).start()
+
+    def fetched(i, which):
+        for k in which:
             own, _, buf = arrays[k]
-            pltpu.make_async_copy(own.at[0], buf.at[slot], load_sem.at[k]).wait()
-
-        span = min(512, tokens)
-
-        @pl.loop(0, tokens // span)
-        def _(step):
-            rows = pl.ds(pl.multiple_of(step * span, span), span)
-            row = normed[rows, :]
-            gate_val = jnp.dot(row, gate_buf[slot], preferred_element_type=jnp.float32)
-            up_val = jnp.dot(row, up_buf[slot], preferred_element_type=jnp.float32)
-            hidden[rows, :] = (jax.nn.silu(gate_val) * up_val).astype(jnp.bfloat16)
-
-        pltpu.make_async_copy(down_in.at[0], down_buf.at[slot], load_sem.at[2]).wait()
-        expert = (zs * CORES + cls) * 2 + j
-
-        @pl.loop(0, tokens // span)
-        def _(step):
-            rows = pl.ds(pl.multiple_of(step * span, span), span)
-            y = jnp.dot(hidden[rows, :], down_buf[slot], preferred_element_type=jnp.float32).astype(jnp.bfloat16).astype(jnp.float32)
-            scale = jnp.concatenate([weight[expert, rows, :]] * (width // LANES), axis=1)
-            total[rows, :] += jnp.where(scale != 0.0, scale * y, 0.0)
+            pltpu.make_async_copy(own.at[0], buf.at[i % 2], load_sem.at[k]).wait()
+
+    span = min(512, tokens)
+
+    @pl.loop(0, items + DEFER)
+    def _(i):
+        at = i - LAG_FROM_Z - (LAG_FROM_XY - LAG_FROM_Z) * relay
+        live = (at >= 1 - relay) & (at < 4 * batches)
+        for k, phase in enumerate((0, 2, 3)):
+            @pl.when(live & ((at + 8) % 4 == phase))
+            def _():
+                exchange((at + 8) // 4 - 2, k)
+
+        late = i - DEFER
+
+        @pl.when(late >= 0)
+        def _():
+            fetch(late, (2,))
+
+        @pl.when(i < items)
+        def _():
+            fetch(i, (0, 1))
+            fetched(i, (0, 1))
+
+            @pl.loop(0, tokens // span)
+            def _(step):
+                rows = pl.ds(pl.multiple_of(step * span, span), span)
+                row = normed[rows, :]
+                gate_val = jnp.dot(row, gate_buf[i % 2], preferred_element_type=jnp.float32)
+                up_val = jnp.dot(row, up_buf[i % 2], preferred_element_type=jnp.float32)
+                hidden[i % 4, rows, :] = (jax.nn.silu(gate_val) * up_val).astype(jnp.bfloat16)
+
+        @pl.when(late >= 0)
+        def _():
+            fetched(late, (2,))
+            _, _, cls, zs, j = locate(late)
+            expert = (zs * CORES + cls) * 2 + j
+
+            @pl.loop(0, tokens // span)
+            def _(step):
+                rows = pl.ds(pl.multiple_of(step * span, span), span)
+                y = jnp.dot(hidden[late % 4, rows, :], down_buf[late % 2], preferred_element_type=jnp.float32).astype(jnp.bfloat16).astype(jnp.float32)
+                lane = lax.broadcasted_iota(jnp.int32, (span, experts), 1)
+                scale = jnp.sum(jnp.where(lane == expert, weight[rows, :], 0.0), axis=1, keepdims=True)
+                total[rows, :] += jnp.where(scale != 0.0, scale * y, 0.0)
 
     @pl.loop(0, tokens // tile)
     def _(step):
@@ -181,8 +201,7 @@
 
     def local_block(x_in, norm_gain, w_router, expert_ids, w_gate, w_up, w_down):
         tokens, width = x_in.shape
-        experts = w_router.shape[1]
-        ff = w_gate.shape[2]
+        experts, ff = w_router.shape[1], w_gate.shape[2]
         batches = nz - 1
         vmem, anywhere = pl.BlockSpec(memory_space=pltpu.VMEM), pl.BlockSpec(memory_space=pl.ANY)
         land_in = jax.ShapeDtypeStruct((CORES, nz, 2, width, ff), jnp.bfloat16)
@@ -190,14 +209,14 @@
         dma = pltpu.SemaphoreType.DMA
         return pl.pallas_call(
             functools.partial(kernel, nz, yspan),
-            out_shape=(jax.ShapeDtypeStruct(x_in.shape, x_in.dtype), land_in, land_in, land_out),
+            out_shape=(pltpu.VMEM(x_in.shape, x_in.dtype), land_in, land_in, land_out),
             in_specs=[vmem, vmem, vmem, vmem, anywhere, anywhere, anywhere],
             out_specs=(vmem, anywhere, anywhere, anywhere),
             scratch_shapes=[
                 pltpu.VMEM((tokens, width), jnp.bfloat16),
                 pltpu.VMEM((tokens, width), jnp.float32),
-                pltpu.VMEM((experts, tokens, LANES), jnp.float32),
-                pltpu.VMEM((tokens, ff), jnp.bfloat16),
+                pltpu.VMEM((tokens, experts), jnp.float32),
+                pltpu.VMEM((4, tokens, ff), jnp.bfloat16),
                 pltpu.VMEM((2, width, ff), jnp.bfloat16),
                 pltpu.VMEM((2, width, ff), jnp.bfloat16),
                 pltpu.VMEM((2, ff, width), jnp.bfloat16),
@@ -209,7 +228,7 @@
             ],
             compiler_params=pltpu.CompilerParams(collective_id=0, has_side_effects=True, vmem_limit_bytes=60 * 1024 * 1024),
             name="moe",
-        )(x_in, norm_gain.reshape(1, width), w_router, expert_ids, w_gate, w_up, w_down)[0]
+        )(x_in, norm_gain, w_router.T, expert_ids.T, w_gate, w_up, w_down)[0]
 
     tok_spec = P(("dp", "ep"), None)
     expert_spec = P("ep", None, None)

time: 288 us -> 287 us (level)
  Pallas kernels: 278 us -> 285 us
  local copies, waits for them, and re-layouts: 7.79 us -> 1.32 us
    pallas_call x1, Pallas kernels: 278 us -> 285 us  [local_block(): pl.pallas_call(functools.partial(kernel, nz, yspan), out_shape=(pltpu.VME...]
    unnamed x3 -> x1, local copies, waits for them, and re-layouts: 6.52 us -> 1.32 us
where the time goes in v2:
time: 287 us; the launch traced here: 286 us
  Pallas kernels  285 us (99%)
    pallas_call x1, Pallas kernels, local_block(): pl.pallas_call(functools.partial(kernel, nz, yspan), out_shape=(pltpu.VME...  285 us

profile of v2, /device:TPU:21, one launch (start us, length us, event | category | flops | bytes accessed | tf_op | source)
XLA Modules:
  0.0 285.9 jit_solution(12291295892034184679)
XLA Ops:
  0.0 284.6 %moe.1 = (bf16[1024,1024]{1,0:T(8,128)(2,1)S(1)}, bf16[2,8,2,1024,512]{4,3,2,1,0:T(8,128)(2,1)}, bf16[2,8,2,1024,512]{4,3,2,1,0:T(8,128)(2,1)}, bf16[2,8,2,512,1024]{4,3,2,1,0:T(8,128)(2,1)}) custom-call(bf16[1024,1024]{1,0:T(8,128)(2,1)} %x_ref.1, bf16[1024]{0:T(1024)(128)(2,1)} %gain_ref.1, bf16[32,1024]{1,0:T(8,128)(2,1)} %bitcast.2, s32[8,1024]{1,0:T(8,128)} %bitcast.3, ...), custom_call_target="tpu_custom_call" | custom-call | tf_op jit(solution)/shard_map/moe/pallas_call | solution.py:210
  284.6 1.3 copy.9

commit v3 on v2

v3 whole, which is shorter than its diff:
```python
import functools
import math

import jax
import jax.numpy as jnp
from jax import lax
from jax.experimental import pallas as pl
from jax.experimental.pallas import tpu as pltpu
from jax.sharding import PartitionSpec as P

EPS = 1e-6
MESH = pl.DeviceIdType.MESH
CORES = 2
DEFER = 4
XY_LAG = 2


def step_times(nz):
    whole = nz // 2 - 1
    slots = 6 * whole + 3
    times = [0, 0, 1, 1]
    for dist in range(1, whole + 1):
        times += [6 * dist - 3] * 2 + [6 * dist - 2] * 2 + [6 * dist - 1] * 2 + [6 * dist] * 2
    return times + [slots - 2] * 2 + [slots] * 4 + [slots + 1] * 2


def kernel(nz, yspan, x_ref, gain_ref, router_ref, ids_ref, gate_in, up_in, down_in, out_ref, gate_land, up_land, down_land,
           normed, total, weight, hidden, gate_buf, up_buf, down_buf, send_z, send_xy, send_sib, recv, recv_sib, load_sem):
    dp, ep = lax.axis_index("dp"), lax.axis_index("ep")
    z, c = ep // CORES, ep % CORES
    a, b = (dp // yspan) % 2, dp % 2
    p = (a + b) % 2
    right = (dp, ((z + 1) % nz) * CORES + c)
    left = (dp, ((z + nz - 1) % nz) * CORES + c)
    x_peer = (dp + yspan * (1 - 2 * a), ep)
    y_peer = (dp + 1 - 2 * b, ep)
    sibling = (dp, z * CORES + 1 - c)
    tokens, width = x_ref.shape
    experts = router_ref.shape[0]
    whole = nz // 2 - 1
    slots = 6 * whole + 3
    items = 4 * nz
    arrays = ((gate_in, gate_land, gate_buf), (up_in, up_land, up_buf), (down_in, down_land, down_buf))

    def send(src, dst, send_sem, recv_sem, device):
        return pltpu.make_async_remote_copy(src_ref=src, dst_ref=dst, send_sem=send_sem, recv_sem=recv_sem, device_id=device, device_id_type=MESH)

    def rows_of(k, piece):
        half = arrays[k][0].shape[1] // 2
        return pl.ds(pl.multiple_of(piece * half, half), half)

    barrier = pltpu.get_barrier_semaphore()
    for peer in (right, left, x_peer, y_peer, sibling):
        pl.semaphore_signal(barrier, inc=1, device_id=peer, device_id_type=MESH)
    pl.semaphore_wait(barrier, 5)

    for k, (own, land, _) in enumerate(arrays):
        for piece in range(2):
            part = rows_of(k, piece)
            for side, peer in enumerate((right, left)):
                send(own.at[p, part], land.at[c, z, p, part], send_z.at[side, 2 * k + piece], recv.at[k, piece, z, p], peer).start()
    for j in range(2):
        for k, (own, land, _) in enumerate(arrays):
            send(own.at[j], land.at[c, z, j], send_sib.at[k, z, j], recv_sib.at[k, z, j], sibling).start()

    tile = min(128, tokens)

    @pl.loop(0, tokens // tile)
    def _(step):
        rows = pl.ds(pl.multiple_of(step * tile, tile), tile)
        resid = x_ref[rows, :].astype(jnp.float32)
        mean_sq = jnp.mean(resid * resid, axis=-1, keepdims=True)
        row = (resid * lax.rsqrt(mean_sq + EPS) * gain_ref[...].astype(jnp.float32).reshape(1, width)).astype(jnp.bfloat16)
        normed[rows, :] = row
        total[rows, :] = resid
        logits = lax.dot_general(router_ref[...], row, (((1,), (1,)), ((), ())), preferred_element_type=jnp.float32)
        ids = ids_ref[:, rows]
        index = lax.broadcasted_iota(jnp.int32, (experts, tile), 0)
        chosen = index == ids[0:1, :]
        for j in range(1, ids.shape[0]):
            chosen = chosen | (index == ids[j:j + 1, :])
        shifted = jnp.exp(logits - jnp.max(logits, axis=0, keepdims=True))
        prob = shifted / jnp.sum(shifted, axis=0, keepdims=True)
        picked = jnp.where(chosen, prob, 0.0)
        gates = picked / jnp.sum(picked, axis=0, keepdims=True)
        weight[rows, :] = gates.T

    def source(side, dist):
        return (z + nz + (2 * side - 1) * dist) % nz

    def take(u, j, from_z):
        is_whole = u < 6 * whole
        at = jnp.where(is_whole, (u % 6) // 2, u - 6 * whole)
        dist = jnp.where(is_whole, 1 + u // 6, whole + 1)
        for k, (own, land, _) in enumerate(arrays):
            @pl.when((u >= 0) & (u < slots) & (at == k))
            def _():
                for side in range(2):
                    zs = source(side, dist)
                    piece = jnp.where(is_whole, u % 2, side)
                    chunk, sem = land.at[c, zs, j, rows_of(k, piece)], recv.at[k, piece, zs, j]
                    send(chunk, chunk, send_z.at[side, u], sem, sibling).wait_recv()
                    if from_z:
                        early = u < 6 * (whole - 1)

                        @pl.when(early | (is_whole & (u % 2 == side)))
                        def _():
                            later = jnp.where(early, u + 6, 6 * whole + (u - 6 * (whole - 1)) // 2)
                            send(chunk, chunk, send_z.at[side, later], sem, (right, left)[side]).start()
                        send(chunk, chunk, send_xy.at[side, u], sem, (x_peer, y_peer)[side]).start()
                for side in range(2):
                    zs = source(side, dist)

                    @pl.when((is_whole & (u % 2 == 1)) | (jnp.logical_not(is_whole) & (side == 0)))
                    def _():
                        send(land.at[c, zs, j], land.at[c, zs, j], send_sib.at[k, zs, j], recv_sib.at[k, zs, j], sibling).start()

    def locate(i):
        m, q = (i + 4) // 8, (i + 4) % 8
        first, last = i < 4, i >= items - 4
        side = q % 2
        other = jnp.where(first, (q - 4) // 2, jnp.where(last, q % 2, (q // 2) % 2))
        dist = jnp.where(first, 0, jnp.where(last, whole + 1, m))
        j = jnp.where(first, side, (p + jnp.where(last, q // 2, q // 4)) % 2)
        return other, first & (other == 0), (c + other) % 2, source(jnp.where(last, 0, side), dist), j

    def fetch(i, which):
        other, native, cls, zs, j = locate(i)

        @pl.when(other == 1)
        def _():
            for k in which:
                own, land, _ = arrays[k]
                send(own.at[0], land.at[cls, zs, j], send_sib.at[k, zs, j], recv_sib.at[k, zs, j], sibling).wait_recv()

        @pl.when(native)
        def _():
            for k in which:
                own, _, buf = arrays[k]
                pltpu.make_async_copy(own.at[j], buf.at[i % 2], load_sem.at[k, i % 2]).start()

        @pl.when(jnp.logical_not(native))
        def _():
            for k in which:
                _, land, buf = arrays[k]
                pltpu.make_async_copy(land.at[cls, zs, j], buf.at[i % 2], load_sem.at[k, i % 2]).start()

    def fetched(i, which):
        for k in which:
            own, _, buf = arrays[k]
            pltpu.make_async_copy(own.at[0], buf.at[i % 2], load_sem.at[k, i % 2]).wait()

    span = min(512, tokens)
    times = step_times(nz)

    def steps_before(v):
        return sum(jnp.where(v > t, times.count(t), 0) for t in sorted(set(times)))

    @pl.loop(0, slots + XY_LAG)
    def _(v):
        take(v, p, True)
        take(v - XY_LAG, 1 - p, False)
        begin, end = steps_before(v), steps_before(v + 1)

        @pl.loop(begin, end)
        def _(i):
            late = i - DEFER

            @pl.when((i == begin) & (i < items))
            def _():
                fetch(i, (0, 1))

            @pl.when(late >= 0)
            def _():
                fetch(late, (2,))

            @pl.when(i < items)
            def _():
                fetched(i, (0, 1))

                @pl.loop(0, tokens // span)
                def _(step):
                    rows = pl.ds(pl.multiple_of(step * span, span), span)
                    row = normed[rows, :]
                    gate_val = jnp.dot(row, gate_buf[i % 2], preferred_element_type=jnp.float32)
                    up_val = jnp.dot(row, up_buf[i % 2], preferred_element_type=jnp.float32)
                    hidden[i % (2 * DEFER), rows, :] = (jax.nn.silu(gate_val) * up_val).astype(jnp.bfloat16)

            @pl.when((i + 1 < end) & (i + 1 < items))
            def _():
                fetch(i + 1, (0, 1))

            @pl.when(late >= 0)
            def _():
                fetched(late, (2,))
                _, _, cls, zs, j = locate(late)
                expert = (zs * CORES + cls) * 2 + j

                @pl.loop(0, tokens // span)
                def _(step):
                    rows = pl.ds(pl.multiple_of(step * span, span), span)
                    y = jnp.dot(hidden[late % (2 * DEFER), rows, :], down_buf[late % 2], preferred_element_type=jnp.float32).astype(jnp.bfloat16).astype(jnp.float32)
                    lane = lax.broadcasted_iota(jnp.int32, (span, experts), 1)
                    scale = jnp.sum(jnp.where(lane == expert, weight[rows, :], 0.0), axis=1, keepdims=True)
                    total[rows, :] += jnp.where(scale != 0.0, scale * y, 0.0)

    @pl.loop(0, tokens // tile)
    def _(step):
        rows = pl.ds(pl.multiple_of(step * tile, tile), tile)
        out_ref[rows, :] = total[rows, :].astype(jnp.bfloat16)

    half = gate_in.at[0, rows_of(0, 0)]

    @pl.loop(0, slots)
    def _(u):
        for side in range(2):
            send(half, half, send_z.at[side, u], recv.at[0, 0, 0, 0], right).wait_send()
            send(half, half, send_xy.at[side, u], recv.at[0, 0, 0, 0], right).wait_send()

    @pl.loop(0, nz)
    def _(zs):
        for k, (own, land, _) in enumerate(arrays):
            for j in range(2):
                send(own.at[0], land.at[0, 0, 0], send_sib.at[k, zs, j], recv_sib.at[k, 0, 0], sibling).wait_send()


def solution(mesh):
    yspan = math.isqrt(mesh.shape["dp"])
    nz = mesh.shape["ep"] // CORES

    def local_block(x_in, norm_gain, w_router, expert_ids, w_gate, w_up, w_down):
        tokens, width = x_in.shape
        experts, ff = w_router.shape[1], w_gate.shape[2]
        slots = 6 * (nz // 2 - 1) + 3
        vmem, anywhere = pl.BlockSpec(memory_space=pltpu.VMEM), pl.BlockSpec(memory_space=pl.ANY)
        land_in = jax.ShapeDtypeStruct((CORES, nz, 2, width, ff), jnp.bfloat16)
        land_out = jax.ShapeDtypeStruct((CORES, nz, 2, ff, width), jnp.bfloat16)
        dma = pltpu.SemaphoreType.DMA
        return pl.pallas_call(
            functools.partial(kernel, nz, yspan),
            out_shape=(pltpu.VMEM(x_in.shape, x_in.dtype), land_in, land_in, land_out),
            in_specs=[vmem, vmem, vmem, vmem, anywhere, anywhere, anywhere],
            out_specs=(vmem, anywhere, anywhere, anywhere),
            scratch_shapes=[
                pltpu.VMEM((tokens, width), jnp.bfloat16),
                pltpu.VMEM((tokens, width), jnp.float32),
                pltpu.VMEM((tokens, experts), jnp.float32),
                pltpu.VMEM((2 * DEFER, tokens, ff), jnp.bfloat16),
                pltpu.VMEM((2, width, ff), jnp.bfloat16),
                pltpu.VMEM((2, width, ff), jnp.bfloat16),
                pltpu.VMEM((2, ff, width), jnp.bfloat16),
                dma((2, slots)),
                dma((2, slots)),
                dma((3, nz, 2)),
                dma((3, 2, nz, 2)),
                dma((3, nz, 2)),
                dma((3, 2)),
            ],
            compiler_params=pltpu.CompilerParams(collective_id=0, has_side_effects=True, vmem_limit_bytes=60 * 1024 * 1024),
            name="moe",
        )(x_in, norm_gain, w_router.T, expert_ids.T, w_gate, w_up, w_down)[0]

    tok_spec = P(("dp", "ep"), None)
    expert_spec = P("ep", None, None)
    return jax.shard_map(local_block, mesh=mesh, in_specs=(tok_spec, P(None), P(None, None), tok_spec, expert_spec, expert_spec, expert_spec), out_specs=tok_spec, check_vma=False)
```

time: 287 us -> 276 us (0.962)
  Pallas kernels: 285 us -> 274 us
    pallas_call x1, Pallas kernels: 285 us -> 274 us  [local_block(): pl.pallas_call(functools.partial(kernel, nz, yspan), out_shape=(pltpu.VME...]
where the time goes in v3:
time: 276 us; the launch traced here: 275 us
  Pallas kernels  274 us (99%)
    pallas_call x1, Pallas kernels, local_block(): pl.pallas_call(functools.partial(kernel, nz, yspan), out_shape=(pltpu.VME...  274 us

profile of v3, /device:TPU:21, one launch (start us, length us, event | category | flops | bytes accessed | tf_op | source)
XLA Modules:
  0.0 275.0 jit_solution(6887430464765957714)
XLA Ops:
  0.0 273.7 %moe.1 = (bf16[1024,1024]{1,0:T(8,128)(2,1)S(1)}, bf16[2,8,2,1024,512]{4,3,2,1,0:T(8,128)(2,1)}, bf16[2,8,2,1024,512]{4,3,2,1,0:T(8,128)(2,1)}, bf16[2,8,2,512,1024]{4,3,2,1,0:T(8,128)(2,1)}) custom-call(bf16[1024,1024]{1,0:T(8,128)(2,1)} %x_ref.1, bf16[1024]{0:T(1024)(128)(2,1)} %gain_ref.1, bf16[32,1024]{1,0:T(8,128)(2,1)} %bitcast.2, s32[8,1024]{1,0:T(8,128)} %bitcast.3, ...), custom_call_target="tpu_custom_call" | custom-call | tf_op jit(solution)/shard_map/moe/pallas_call | solution.py:239
  273.7 1.3 copy.9

commit v4 on v3

--- a/solution.py
+++ b/solution.py
@@ -18,14 +18,15 @@
 def step_times(nz):
     whole = nz // 2 - 1
     slots = 6 * whole + 3
-    times = [0, 0, 1, 1]
+    times = [0, 0, 1, 2]
     for dist in range(1, whole + 1):
-        times += [6 * dist - 3] * 2 + [6 * dist - 2] * 2 + [6 * dist - 1] * 2 + [6 * dist] * 2
-    return times + [slots - 2] * 2 + [slots] * 4 + [slots + 1] * 2
+        spread = (0, 1, 2, 2, 3, 4, 4, 5) if dist < whole else (0, 0, 1, 1, 2, 2, 3, 3)
+        times += [6 * dist - 3 + after for after in spread]
+    return times + [slots - 2] * 3 + [slots - 1] * 2 + [slots] * 2 + [slots + 1] * 2
 
 
 def kernel(nz, yspan, x_ref, gain_ref, router_ref, ids_ref, gate_in, up_in, down_in, out_ref, gate_land, up_land, down_land,
-           normed, total, weight, hidden, gate_buf, up_buf, down_buf, send_z, send_xy, send_sib, recv, recv_sib, load_sem):
+           normed, total, weight, hidden, gate_buf, up_buf, down_buf, x_buf, send_z, send_xy, send_sib, send_extra, recv, recv_sib, recv_extra, load_sem, x_sem):
     dp, ep = lax.axis_index("dp"), lax.axis_index("ep")
     z, c = ep // CORES, ep % CORES
     a, b = (dp // yspan) % 2, dp % 2
@@ -49,6 +50,12 @@
         half = arrays[k][0].shape[1] // 2
         return pl.ds(pl.multiple_of(piece * half, half), half)
 
+    x_load = pltpu.make_async_copy(x_ref, x_buf, x_sem)
+    x_load.start()
+    def quarter(piece, part):
+        size = down_in.shape[1] // 4
+        return pl.ds((2 * piece + part) * size, size)
+
     barrier = pltpu.get_barrier_semaphore()
     for peer in (right, left, x_peer, y_peer, sibling):
         pl.semaphore_signal(barrier, inc=1, device_id=peer, device_id_type=MESH)
@@ -64,11 +71,12 @@
             send(own.at[j], land.at[c, z, j], send_sib.at[k, z, j], recv_sib.at[k, z, j], sibling).start()
 
     tile = min(128, tokens)
+    x_load.wait()
 
     @pl.loop(0, tokens // tile)
     def _(step):
         rows = pl.ds(pl.multiple_of(step * tile, tile), tile)
-        resid = x_ref[rows, :].astype(jnp.float32)
+        resid = x_buf[rows, :].astype(jnp.float32)
         mean_sq = jnp.mean(resid * resid, axis=-1, keepdims=True)
         row = (resid * lax.rsqrt(mean_sq + EPS) * gain_ref[...].astype(jnp.float32).reshape(1, width)).astype(jnp.bfloat16)
         normed[rows, :] = row
@@ -93,7 +101,7 @@
         at = jnp.where(is_whole, (u % 6) // 2, u - 6 * whole)
         dist = jnp.where(is_whole, 1 + u // 6, whole + 1)
         for k, (own, land, _) in enumerate(arrays):
-            @pl.when((u >= 0) & (u < slots) & (at == k))
+            @pl.when((u >= 0) & (u < slots - 1) & (at == k))
             def _():
                 for side in range(2):
                     zs = source(side, dist)
@@ -114,6 +122,31 @@
                     @pl.when((is_whole & (u % 2 == 1)) | (jnp.logical_not(is_whole) & (side == 0)))
                     def _():
                         send(land.at[c, zs, j], land.at[c, zs, j], send_sib.at[k, zs, j], recv_sib.at[k, zs, j], sibling).start()
+
+    def take_last(j, from_z):
+        _, land, _ = arrays[2]
+        zs = source(0, whole + 1)
+
+        def share(part):
+            send(part, part, send_sib.at[2, zs, j], recv_sib.at[2, zs, j], sibling).start()
+
+        for side in range(2):
+            sem, first = recv.at[2, side, zs, j], land.at[c, zs, j, quarter(side, 0)]
+            if from_z:
+                chunk = land.at[c, zs, j, rows_of(2, side)]
+                send(chunk, chunk, send_z.at[side, 0], sem, sibling).wait_recv()
+                send(first, first, send_xy.at[side, slots - 1], sem, (x_peer, y_peer)[side]).start()
+                extra = land.at[c, source(side, whole), 1 - j, quarter(side, 1)]
+                send(extra, extra, send_extra.at[side], recv_extra.at[side], (right, left)[side]).start()
+                share(chunk)
+            else:
+                send(first, first, send_z.at[side, 0], sem, sibling).wait_recv()
+                share(first)
+        if not from_z:
+            for side in range(2):
+                second = land.at[c, zs, j, quarter(side, 1)]
+                send(second, second, send_z.at[side, 0], recv_extra.at[side], sibling).wait_recv()
+                share(second)
 
     def locate(i):
         m, q = (i + 4) // 8, (i + 4) % 8
@@ -150,7 +183,7 @@
             own, _, buf = arrays[k]
             pltpu.make_async_copy(own.at[0], buf.at[i % 2], load_sem.at[k, i % 2]).wait()
 
-    span = min(512, tokens)
+    span = min(1024, tokens)
     times = step_times(nz)
 
     def steps_before(v):
@@ -159,46 +192,62 @@
     @pl.loop(0, slots + XY_LAG)
     def _(v):
         take(v, p, True)
+
+        @pl.when(v == slots - 1)
+        def _():
+            take_last(p, True)
         take(v - XY_LAG, 1 - p, False)
+
+        @pl.when(v - XY_LAG == slots - 1)
+        def _():
+            take_last(1 - p, False)
         begin, end = steps_before(v), steps_before(v + 1)
 
         @pl.loop(begin, end)
-        def _(i):
-            late = i - DEFER
-
-            @pl.when((i == begin) & (i < items))
+        def _(step):
+            tail = step - (items - 4)
+            i = jnp.where(tail <= 0, step, jnp.where(tail == 3, items - 3, step - 3))
+            early = (tail <= 0) | (tail == 3) | (tail == 5) | (tail == 6)
+            late = jnp.where(tail <= 4, step - DEFER, step - DEFER - 1)
+            ripe = (late >= 0) & (tail != 5)
+
+            @pl.when(early & ((tail > 0) | ((step == begin) & (i % 4 == 0))))
             def _():
                 fetch(i, (0, 1))
 
-            @pl.when(late >= 0)
+            @pl.when(ripe & (tail != 1) & (tail != 2) & (tail != 4))
             def _():
                 fetch(late, (2,))
 
-            @pl.when(i < items)
+            @pl.when(early)
             def _():
                 fetched(i, (0, 1))
 
                 @pl.loop(0, tokens // span)
-                def _(step):
-                    rows = pl.ds(pl.multiple_of(step * span, span), span)
+                def _(part):
+                    rows = pl.ds(pl.multiple_of(part * span, span), span)
                     row = normed[rows, :]
                     gate_val = jnp.dot(row, gate_buf[i % 2], preferred_element_type=jnp.float32)
                     up_val = jnp.dot(row, up_buf[i % 2], preferred_element_type=jnp.float32)
                     hidden[i % (2 * DEFER), rows, :] = (jax.nn.silu(gate_val) * up_val).astype(jnp.bfloat16)
 
-            @pl.when((i + 1 < end) & (i + 1 < items))
+            @pl.when((tail < 0) & ((step + 1 < end) | ((i + 1) % 4 != 0)))
             def _():
                 fetch(i + 1, (0, 1))
 
-            @pl.when(late >= 0)
+            @pl.when((tail == 0) | (tail == 1) | (tail == 3))
+            def _():
+                fetch(late + 1, (2,))
+
+            @pl.when(ripe)
             def _():
                 fetched(late, (2,))
                 _, _, cls, zs, j = locate(late)
                 expert = (zs * CORES + cls) * 2 + j
 
                 @pl.loop(0, tokens // span)
-                def _(step):
-                    rows = pl.ds(pl.multiple_of(step * span, span), span)
+                def _(part):
+                    rows = pl.ds(pl.multiple_of(part * span, span), span)
                     y = jnp.dot(hidden[late % (2 * DEFER), rows, :], down_buf[late % 2], preferred_element_type=jnp.float32).astype(jnp.bfloat16).astype(jnp.float32)
                     lane = lax.broadcasted_iota(jnp.int32, (span, experts), 1)
                     scale = jnp.sum(jnp.where(lane == expert, weight[rows, :], 0.0), axis=1, keepdims=True)
@@ -215,7 +264,15 @@
     def _(u):
         for side in range(2):
             send(half, half, send_z.at[side, u], recv.at[0, 0, 0, 0], right).wait_send()
-            send(half, half, send_xy.at[side, u], recv.at[0, 0, 0, 0], right).wait_send()
+
+            @pl.when(u < slots - 1)
+            def _():
+                send(half, half, send_xy.at[side, u], recv.at[0, 0, 0, 0], right).wait_send()
+
+    piece = down_in.at[0, quarter(0, 0)]
+    for side in range(2):
+        send(piece, piece, send_xy.at[side, slots - 1], recv.at[0, 0, 0, 0], right).wait_send()
+        send(piece, piece, send_extra.at[side], recv.at[0, 0, 0, 0], right).wait_send()
 
     @pl.loop(0, nz)
     def _(zs):
@@ -239,7 +296,7 @@
         return pl.pallas_call(
             functools.partial(kernel, nz, yspan),
             out_shape=(pltpu.VMEM(x_in.shape, x_in.dtype), land_in, land_in, land_out),
-            in_specs=[vmem, vmem, vmem, vmem, anywhere, anywhere, anywhere],
+            in_specs=[anywhere, vmem, vmem, vmem, anywhere, anywhere, anywhere],
             out_specs=(vmem, anywhere, anywhere, anywhere),
             scratch_shapes=[
                 pltpu.VMEM((tokens, width), jnp.bfloat16),
@@ -249,12 +306,16 @@
                 pltpu.VMEM((2, width, ff), jnp.bfloat16),
                 pltpu.VMEM((2, width, ff), jnp.bfloat16),
                 pltpu.VMEM((2, ff, width), jnp.bfloat16),
+                pltpu.VMEM((tokens, width), jnp.bfloat16),
                 dma((2, slots)),
                 dma((2, slots)),
                 dma((3, nz, 2)),
+                dma((2,)),
                 dma((3, 2, nz, 2)),
                 dma((3, nz, 2)),
+                dma((2,)),
                 dma((3, 2)),
+                dma(()),
             ],
             compiler_params=pltpu.CompilerParams(collective_id=0, has_side_effects=True, vmem_limit_bytes=60 * 1024 * 1024),
             name="moe",

time: 276 us -> 274 us (level)
  no operation moved by 1% of the time
where the time goes in v4:
time: 274 us; the launch traced here: 273 us
  Pallas kernels  272 us (99%)
    pallas_call x1, Pallas kernels, local_block(): pl.pallas_call(functools.partial(kernel, nz, yspan), out_shape=(pltpu.VME...  272 us

profile of v4, /device:TPU:21, one launch (start us, length us, event | category | flops | bytes accessed | tf_op | source)
XLA Modules:
  0.0 273.2 jit_solution(7461037950065946786)
XLA Ops:
  0.0 271.9 %moe.1 = (bf16[1024,1024]{1,0:T(8,128)(2,1)S(1)}, bf16[2,8,2,1024,512]{4,3,2,1,0:T(8,128)(2,1)}, bf16[2,8,2,1024,512]{4,3,2,1,0:T(8,128)(2,1)}, bf16[2,8,2,512,1024]{4,3,2,1,0:T(8,128)(2,1)}) custom-call(bf16[1024,1024]{1,0:T(8,128)(2,1)} %x_ref.1, bf16[1024]{0:T(1024)(128)(2,1)} %gain_ref.1, bf16[32,1024]{1,0:T(8,128)(2,1)} %bitcast.2, s32[8,1024]{1,0:T(8,128)} %bitcast.3, ...), custom_call_target="tpu_custom_call" | custom-call | tf_op jit(solution)/shard_map/moe/pallas_call | solution.py:296
  271.9 1.3 copy.9
